TPU v7x, 32 devices: a whole 2x2x4 slice. The times are simulated.
32 devices in a mesh: fsdp: 4 (over y, x), tp: 8 (over z, core).
Axes of the slice: x: 2, y: 2, z: 4, core: 2. Of those that a mesh axis runs over, the one named last changes fastest.
Arguments:
- tokens: bfloat16 [1024, 8192], P('fsdp', 'tp'), may hold values from -6 to 6
- out_grad: bfloat16 [1024, 8192], P('fsdp', 'tp'), may hold values from -6 to 6
- gate_weight: bfloat16 [8192, 1024], P('fsdp', 'tp'), may hold values from -0.0625 to 0.0625
- up_weight: bfloat16 [8192, 1024], P('fsdp', 'tp'), may hold values from -0.0625 to 0.0625
- down_weight: bfloat16 [1024, 8192], P('tp', 'fsdp'), may hold values from -0.1875 to 0.1875
Outputs:
- input_grad: bfloat16 [1024, 8192], P('fsdp', 'tp')
- gate_grad: float32 [8192, 1024], P('fsdp', 'tp')
- up_grad: float32 [8192, 1024], P('fsdp', 'tp')
- down_grad: float32 [1024, 8192], P('tp', 'fsdp')
All inputs are finite; a program needn't handle non-finite values.
Results may differ from a plain program's by a relative error of at most 0.0023.
Values may be sent and summed in bfloat16 or wider, within the bound.
A program may use at most 128 MiB of HBM per device.

v0:
```python
import math
import jax
import jax.numpy as jnp
from jax import lax
from jax.sharding import PartitionSpec as P


def over_all(shard, axis, dim, absorb, state):
    everything = jax.tree.map(lambda a: lax.all_gather(a, axis, axis=dim, tiled=True), shard)
    return absorb(state, everything, jnp.int32(0))


def own_rows(portion, rows, axis):
    count = rows * lax.axis_size(axis)
    return lax.psum_scatter(portion(jnp.int32(0), count), axis, scatter_dimension=0, tiled=True)


def column_term(left, right, start, count, factor):
    block = lax.dynamic_slice_in_dim(left, start, count, 1)
    product = lax.dot_general(
        block, right, (((0,), (0,)), ((), ())), preferred_element_type=jnp.float32
    )
    return product * factor


def body(tokens, out_grad, gate_weight, up_weight, down_weight):
    factor = 1.0 / math.sqrt(tokens.shape[0] * lax.axis_size("fsdp"))
    whole = lax.all_gather(tokens, "tp", axis=1, tiled=True)
    grads = lax.all_gather(out_grad, "tp", axis=1, tiled=True)
    gate_full, up_full = (
        lax.all_gather(gate_weight, "fsdp", axis=0, tiled=True),
        lax.all_gather(up_weight, "fsdp", axis=0, tiled=True),
    )
    gate = jnp.dot(whole, gate_full, preferred_element_type=jnp.float32)
    up = jnp.dot(whole, up_full, preferred_element_type=jnp.float32)

    def add_down(total, piece, start):
        columns = lax.dynamic_slice_in_dim(grads, start, piece.shape[1], 1)
        return total + lax.dot_general(
            columns, piece, (((1,), (1,)), ((), ())), preferred_element_type=jnp.float32
        )

    initial = jnp.zeros((whole.shape[0], down_weight.shape[0]), jnp.float32)
    hidden_grad = over_all(down_weight, "fsdp", 1, add_down, initial)
    squashed = jax.nn.sigmoid(gate)
    activated = gate * squashed
    slope = squashed * (1.0 + gate * (1.0 - squashed))
    hidden = (activated * up).astype(jnp.bfloat16)
    gate_delta = (hidden_grad * up * slope).astype(jnp.bfloat16)
    up_delta = (hidden_grad * activated).astype(jnp.bfloat16)
    partial_term = jnp.dot(gate_delta, gate_full.T, preferred_element_type=jnp.float32)
    partial_term = partial_term + jnp.dot(up_delta, up_full.T, preferred_element_type=jnp.float32)
    input_grad = lax.psum_scatter(partial_term, "tp", scatter_dimension=1, tiled=True).astype(
        jnp.bfloat16
    )
    rows_here = gate_weight.shape[0]

    def joint_term(start, count):
        return jnp.concatenate(
            [
                column_term(whole, gate_delta, start, count, factor),
                column_term(whole, up_delta, start, count, factor),
                column_term(grads, hidden, start, count, factor),
            ],
            axis=1,
        )

    summed = own_rows(joint_term, rows_here, "fsdp")
    width = gate_delta.shape[1]
    gate_grad = summed[:, :width]
    up_grad = summed[:, width : 2 * width]
    down_grad = summed[:, 2 * width :].T
    return (input_grad, gate_grad, up_grad, down_grad)


def solution(mesh):
    return jax.shard_map(
        body,
        mesh=mesh,
        in_specs=(
            P("fsdp", "tp"),
            P("fsdp", "tp"),
            P("fsdp", "tp"),
            P("fsdp", "tp"),
            P("tp", "fsdp"),
        ),
        out_specs=(P("fsdp", "tp"), P("fsdp", "tp"), P("fsdp", "tp"), P("tp", "fsdp")),
        check_vma=False,
    )
```

profile of v0, /device:TPU:0, one launch (start us, length us, event | category | flops | bytes accessed | tf_op | source)
XLA Modules:
  0.0 450.8 jit_solution(9459281939705098741)
XLA Ops:
  7.2 0.0 all-gather.14.cloned.1.call-start
  7.2 0.7 all-gather.14.cloned.1.call-update
  7.9 0.0 all-gather.10.cloned.1.call-start
  7.9 0.7 all-gather.10.cloned.1.call-update
  8.6 0.0 all-gather.12.cloned.1.call-start
  8.7 0.7 all-gather.12.cloned.1.call-update
  9.4 0.0 all-gather.8.cloned.1.call-start
  9.4 0.5 all-gather.8.cloned.1.call-update
  10.0 0.0 all-gather.6.cloned.1.call-start
  10.0 0.5 all-gather.6.cloned.1.call-update
  10.5 0.0 reduce-scatter.3.cloned.1.call-start
  10.6 37.2 %all-gather.14.cloned.1.call-done = bf16[8192,128]{1,0:T(8,128)(2,1)} async-done(((bf16[2048,128]{1,0:T(8,128)(2,1)}), bf16[8192,128]{1,0:T(8,128)(2,1)}) %all-gather.14.cloned.1.call-update) | async-done | bytes 2097168 | tf_op jit(solution)/shard_map/all_gather | solution.py:31
  47.8 48.5 %all-gather.10.cloned.1.call-done = bf16[256,8192]{1,0:T(8,128)(2,1)} async-done(((bf16[256,1024]{1,0:T(8,128)(2,1)}), bf16[256,8192]{1,0:T(8,128)(2,1)}) %all-gather.10.cloned.1.call-update) | async-done | bytes 4194320 | tf_op jit(solution)/shard_map/all_gather | solution.py:28
  96.3 4.1 fusion.7
  100.4 31.8 %all-gather.12.cloned.1.call-done = bf16[8192,128]{1,0:T(8,128)(2,1)} async-done(((bf16[2048,128]{1,0:T(8,128)(2,1)}), bf16[8192,128]{1,0:T(8,128)(2,1)}) %all-gather.12.cloned.1.call-update) | async-done | bytes 2097168 | tf_op jit(solution)/shard_map/all_gather | solution.py:32
  132.1 4.1 fusion.6
  136.2 0.0 copy-start.1
  136.2 32.8 %all-gather.8.cloned.1.call-done = bf16[128,8192]{1,0:T(8,128)(2,1)} async-done(((bf16[128,2048]{1,0:T(8,128)(2,1)}), bf16[128,8192]{1,0:T(8,128)(2,1)}) %all-gather.8.cloned.1.call-update) | async-done | bytes 2097168 | tf_op jit(solution)/shard_map/all_gather | solution.py:9
  169.0 48.4 %all-gather.6.cloned.1.call-done = bf16[256,8192]{1,0:T(8,128)(2,1)} async-done(((bf16[256,1024]{1,0:T(8,128)(2,1)}), bf16[256,8192]{1,0:T(8,128)(2,1)}) %all-gather.6.cloned.1.call-update) | async-done | bytes 4194320 | tf_op jit(solution)/shard_map/all_gather | solution.py:29
  217.4 4.1 multiply_convert_fusion.1
  221.5 0.0 copy-done.1
  221.5 0.0 copy-start.2
  221.5 1.3 fusion.8
  222.8 0.3 copy-done.2
  223.1 4.5 convolution_add_fusion
  227.6 0.0 reduce-scatter.3.cloned.1.call-update
  227.6 0.0 reduce-scatter.5.cloned.1.call-start
  227.6 0.0 copy-start
  227.6 3.1 fusion.1
  230.8 0.3 copy-done
  231.1 0.0 copy-start.3
  231.1 0.8 fusion.2
  231.9 2.1 copy-done.3
  234.0 0.8 fusion
  234.8 5.0 %pad_maximum_fusion = f32[8192,384]{0,1:T(8,128)} fusion(f32[8192,128]{0,1:T(8,128)S(1)} %fusion, f32[8192,128]{0,1:T(8,128)S(1)} %fusion.1, f32[8192,128]{0,1:T(8,128)S(1)} %fusion.2), kind=kLoop, calls=%fused_computation | loop fusion | flops 6291456 | bytes 25165824 | tf_op jit(solution)/shard_map/concatenate | solution.py:59
  239.8 0.0 reduce-scatter.5.cloned.1.call-update
  239.9 76.2 %reduce-scatter.3.cloned.1.call-done = f32[256,1024]{1,0:T(8,128)} async-done(((f32[256,8192]{1,0:T(8,128)}), f32[256,1024]{1,0:T(8,128)}) %reduce-scatter.3.cloned.1.call-update) | async-done | bytes 1048592 | tf_op jit(solution)/shard_map/reduce_scatter | solution.py:53
  316.1 2.1 convert_element_type.14
  318.2 120.1 %reduce-scatter.5.cloned.1.call-done = f32[2048,384]{0,1:T(8,128)} async-done(((f32[8192,384]{0,1:T(8,128)}), f32[2048,384]{0,1:T(8,128)}) %reduce-scatter.5.cloned.1.call-update) | async-done | bytes 3145744 | tf_op jit(solution)/shard_map/reduce_scatter | solution.py:15
  438.3 3.1 slice_bitcast_fusion
  441.4 1.3 copy.9
  442.7 1.3 copy.10
Async XLA Ops:
  7.2 40.6 %all-gather.14.cloned.1.call-start = ((), (), s32[]{:S(2)}) async-start(), calls=%async_computation.6 | async-start | bytes 2621440 | tf_op jit(solution)/shard_map/all_gather | solution.py:31
  7.9 88.4 %all-gather.10.cloned.1.call-start = ((), (), s32[]{:S(2)}) async-start(), calls=%async_computation.4 | async-start | bytes 4718592 | tf_op jit(solution)/shard_map/all_gather | solution.py:28
  8.6 123.5 %all-gather.12.cloned.1.call-start = ((), (), s32[]{:S(2)}) async-start(), calls=%async_computation.5 | async-start | bytes 2621440 | tf_op jit(solution)/shard_map/all_gather | solution.py:32
  9.4 159.6 %all-gather.8.cloned.1.call-start = ((), (), s32[]{:S(2)}) async-start(), calls=%async_computation.3 | async-start | bytes 2621440 | tf_op jit(solution)/shard_map/all_gather | solution.py:9
  10.0 207.4 %all-gather.6.cloned.1.call-start = ((), (), s32[]{:S(2)}) async-start(), calls=%async_computation.2 | async-start | bytes 4718592 | tf_op jit(solution)/shard_map/all_gather | solution.py:29
  10.5 305.5 %reduce-scatter.3.cloned.1.call-start = ((), (), s32[]{:S(2)}) async-start(), calls=%async_computation.7 | async-start | bytes 9437184 | tf_op jit(solution)/shard_map/reduce_scatter | solution.py:53
  136.2 85.3 %copy-start.1 = (bf16[8192,128]{1,0:T(8,128)(2,1)S(1)}, bf16[8192,128]{1,0:T(8,128)(2,1)}, u32[]{:S(2)}) copy-start(bf16[8192,128]{1,0:T(8,128)(2,1)} %all-gather.14.cloned.1.call-done) | copy-start | bytes 6291460
  221.5 1.6 copy-start.2
  227.6 210.7 %reduce-scatter.5.cloned.1.call-start = ((), (), s32[]{:S(2)}) async-start(), calls=%async_computation.8 | async-start | bytes 15728640 | tf_op jit(solution)/shard_map/reduce_scatter | solution.py:15
  227.6 3.5 copy-start
  231.1 2.9 copy-start.3
Sparse Core Ops, SparseCore 0:
  9.8 37.8 all-gather.13
  49.4 46.8 all-gather.9
  98.1 33.9 all-gather.11
  133.8 35.1 all-gather.7
  170.5 46.8 all-gather.5
  227.7 88.3 reduce-scatter.2
  319.2 119.0 reduce-scatter.4
where the time goes:
time: 451 us
  waiting for transfers between devices  398 us (88%)
  matrix products  22.8 us (5%)
  between operations  14.2 us (3%)
  local copies, waits for them, and re-layouts  8.46 us (2%)
  other arithmetic  7.1 us (2%)
    reduce_scatter x1, waiting for transfers between devices, own_rows(): lax.psum_scatter(portion(jnp.int32(0), count), axis, scatter_dimension=0,...  120 us
    reduce_scatter x1, waiting for transfers between devices, body(): lax.psum_scatter(partial_term, 'tp', scatter_dimension=1, tiled=True)  76.2 us
    all_gather x1, waiting for transfers between devices, body(): whole = lax.all_gather(tokens, 'tp', axis=1, tiled=True)  48.5 us
    all_gather x1, waiting for transfers between devices, body(): grads = lax.all_gather(out_grad, 'tp', axis=1, tiled=True)  48.4 us
    all_gather x1, waiting for transfers between devices, body(): lax.all_gather(gate_weight, 'fsdp', axis=0, tiled=True)  37.2 us
    all_gather x1, waiting for transfers between devices, over_all(): lax.all_gather(a, axis, axis=dim, tiled=True)  32.8 us
    all_gather x1, waiting for transfers between devices, body(): lax.all_gather(up_weight, 'fsdp', axis=0, tiled=True)  31.8 us
  transfers between devices with their start and end apart: 7, of which 7 were waited for; matrix products, arithmetic and copies ran while one was open for 4% of the time, Pallas kernels for 0%

commit v1 on v0

--- a/solution.py
+++ b/solution.py
@@ -26,7 +26,12 @@
 def body(tokens, out_grad, gate_weight, up_weight, down_weight):
     factor = 1.0 / math.sqrt(tokens.shape[0] * lax.axis_size("fsdp"))
     whole = lax.all_gather(tokens, "tp", axis=1, tiled=True)
-    grads = lax.all_gather(out_grad, "tp", axis=1, tiled=True)
+    ring = [out_grad]
+    for hop in range(7):
+        ring.append(lax.ppermute(ring[-1], "tp", [(dev, (dev + 1) % 8) for dev in range(8)]))
+    grads = jnp.roll(
+        jnp.concatenate(ring[::-1], axis=1), (lax.axis_index("tp") + 1) * ring[0].shape[1], axis=1
+    )
     gate_full, up_full = (
         lax.all_gather(gate_weight, "fsdp", axis=0, tiled=True),
         lax.all_gather(up_weight, "fsdp", axis=0, tiled=True),

time: 451 us -> 417 us (0.925)
  waiting for transfers between devices: 398 us -> 347 us
  local copies, waits for them, and re-layouts: 8.46 us -> 23.8 us
    ppermute x0 -> x7, waiting for transfers between devices: none -> 97.1 us  [body(): lax.ppermute(ring[-1], 'tp', [(dev, (dev + 1) % 8) for dev in range(8)])]
    all_gather x1, waiting for transfers between devices: 48.5 us -> 0.01 us  [body(): whole = lax.all_gather(tokens, 'tp', axis=1, tiled=True)]
    all_gather x1 -> x0, waiting for transfers between devices: 48.4 us -> none  [body(): grads = lax.all_gather(out_grad, 'tp', axis=1, tiled=True)]
    all_gather x1, waiting for transfers between devices: 31.8 us -> 0.01 us  [body(): lax.all_gather(up_weight, 'fsdp', axis=0, tiled=True)]
    all_gather x1, waiting for transfers between devices: 37.2 us -> 15.7 us  [body(): lax.all_gather(gate_weight, 'fsdp', axis=0, tiled=True)]
    unnamed x10 -> x23, local copies, waits for them, and re-layouts: 5.38 us -> 19.9 us
  transfers between devices with their start and end apart: 7 -> 13, of which waited for: 7 -> 11; matrix products, arithmetic and copies ran while one was open for 4% -> 9% of each run, Pallas kernels for 0% -> 0%
where the time goes in v1:
time: 417 us
  waiting for transfers between devices  347 us (83%)
  matrix products  24.4 us (6%)
  local copies, waits for them, and re-layouts  23.8 us (6%)
  between operations  14.2 us (3%)
  other arithmetic  7.07 us (2%)
    reduce_scatter x1, waiting for transfers between devices, own_rows(): lax.psum_scatter(portion(jnp.int32(0), count), axis, scatter_dimension=0,...  120 us
    ppermute x7, waiting for transfers between devices, body(): lax.ppermute(ring[-1], 'tp', [(dev, (dev + 1) % 8) for dev in range(8)])  97.1 us
    reduce_scatter x1, waiting for transfers between devices, body(): lax.psum_scatter(partial_term, 'tp', scatter_dimension=1, tiled=True)  79.6 us
    all_gather x1, waiting for transfers between devices, over_all(): lax.all_gather(a, axis, axis=dim, tiled=True)  32.8 us
    unnamed x23, local copies, waits for them, and re-layouts  19.9 us
    all_gather x1, waiting for transfers between devices, body(): lax.all_gather(gate_weight, 'fsdp', axis=0, tiled=True)  15.7 us
  transfers between devices with their start and end apart: 13, of which 11 were waited for; matrix products, arithmetic and copies ran while one was open for 9% of the time, Pallas kernels for 0%

profile of v1, /device:TPU:0, one launch (start us, length us, event | category | flops | bytes accessed | tf_op | source)
XLA Modules:
  0.0 417.0 jit_solution(7089358789763589093)
XLA Ops:
  7.2 0.0 copy-start.2
  7.2 0.0 all-gather.9.cloned.1.call-start
  7.2 0.7 all-gather.9.cloned.1.call-update
  7.9 0.0 all-gather.7.cloned.1.call-start
  8.0 0.7 all-gather.7.cloned.1.call-update
  8.7 0.0 all-gather.11.cloned.1.call-start
  8.7 0.5 collective-permute-start
  9.2 0.1 all-gather.11.cloned.1.call-update
  9.4 0.0 all-gather.5.cloned.1.call-start
  9.4 10.9 %collective-permute-done = bf16[256,1024]{1,0:T(8,128)(2,1)S(1)} collective-permute-done((bf16[256,1024]{1,0:T(8,128)(2,1)}, bf16[256,1024]{1,0:T(8,128)(2,1)S(1)}, u32[]{:S(2)}, u32[]{:S(2)}) %collective-permute-start) | collective-permute-done | bytes 524320 | tf_op jit(solution)/shard_map/ppermute | solution.py:31
  20.4 0.0 collective-permute-start.1
  20.4 10.4 %collective-permute-done.1 = bf16[256,1024]{1,0:T(8,128)(2,1)S(1)} collective-permute-done((bf16[256,1024]{1,0:T(8,128)(2,1)S(1)}, bf16[256,1024]{1,0:T(8,128)(2,1)S(1)}, u32[]{:S(2)}, u32[]{:S(2)}) %collective-permute-start.1) | collective-permute-done | bytes 524320 | tf_op jit(solution)/shard_map/ppermute | solution.py:31
  30.8 0.0 collective-permute-start.2
  30.8 10.4 %collective-permute-done.2 = bf16[256,1024]{1,0:T(8,128)(2,1)S(1)} collective-permute-done((bf16[256,1024]{1,0:T(8,128)(2,1)S(1)}, bf16[256,1024]{1,0:T(8,128)(2,1)S(1)}, u32[]{:S(2)}, u32[]{:S(2)}) %collective-permute-start.2) | collective-permute-done | bytes 524320 | tf_op jit(solution)/shard_map/ppermute | solution.py:31
  41.2 0.0 collective-permute-start.3
  41.2 10.4 %collective-permute-done.3 = bf16[256,1024]{1,0:T(8,128)(2,1)S(1)} collective-permute-done((bf16[256,1024]{1,0:T(8,128)(2,1)S(1)}, bf16[256,1024]{1,0:T(8,128)(2,1)S(1)}, u32[]{:S(2)}, u32[]{:S(2)}) %collective-permute-start.3) | collective-permute-done | bytes 524320 | tf_op jit(solution)/shard_map/ppermute | solution.py:31
  51.6 0.0 collective-permute-start.4
  51.6 11.1 %collective-permute-done.4 = bf16[256,1024]{1,0:T(8,128)(2,1)S(1)} collective-permute-done((bf16[256,1024]{1,0:T(8,128)(2,1)S(1)}, bf16[256,1024]{1,0:T(8,128)(2,1)S(1)}, u32[]{:S(2)}, u32[]{:S(2)}) %collective-permute-start.4) | collective-permute-done | bytes 524320 | tf_op jit(solution)/shard_map/ppermute | solution.py:31
  62.7 0.0 collective-permute-start.5
  62.7 21.9 %collective-permute-done.5 = bf16[256,1024]{1,0:T(8,128)(2,1)} collective-permute-done((bf16[256,1024]{1,0:T(8,128)(2,1)S(1)}, bf16[256,1024]{1,0:T(8,128)(2,1)}, u32[]{:S(2)}, u32[]{:S(2)}) %collective-permute-start.5) | collective-permute-done | bytes 524320 | tf_op jit(solution)/shard_map/ppermute | solution.py:31
  84.5 0.0 collective-permute-start.6
  84.5 0.0 all-gather.5.cloned.1.call-update
  84.6 0.0 reduce-scatter.3.cloned.1.call-start
  84.6 22.0 %collective-permute-done.6 = bf16[256,1024]{1,0:T(8,128)(2,1)} collective-permute-done((bf16[256,1024]{1,0:T(8,128)(2,1)}, bf16[256,1024]{1,0:T(8,128)(2,1)}, u32[]{:S(2)}, u32[]{:S(2)}) %collective-permute-start.6) | collective-permute-done | bytes 524320 | tf_op jit(solution)/shard_map/ppermute | solution.py:31
  106.6 1.9 constant_dynamic-update-slice_fusion.15
  108.5 1.9 constant_dynamic-update-slice_fusion.14
  110.4 0.9 constant_dynamic-update-slice_fusion.13
  111.2 0.8 constant_dynamic-update-slice_fusion.12
  112.1 0.8 constant_dynamic-update-slice_fusion.11
  112.9 0.9 constant_dynamic-update-slice_fusion.10
  113.8 0.8 constant_dynamic-update-slice_fusion.9
  114.6 0.0 copy-done.2
  114.6 0.9 constant_dynamic-update-slice_fusion.8
  115.5 1.9 constant_dynamic-update-slice_fusion.7
  117.4 1.9 constant_dynamic-update-slice_fusion.6
  119.4 0.9 constant_dynamic-update-slice_fusion.5
  120.2 0.8 constant_dynamic-update-slice_fusion.4
  121.1 0.8 constant_dynamic-update-slice_fusion.3
  121.9 0.8 constant_dynamic-update-slice_fusion.2
  122.8 0.9 constant_dynamic-update-slice_fusion.1
  123.6 0.9 constant_dynamic-update-slice_fusion
  124.5 4.1 fusion.10
  128.6 15.7 %all-gather.11.cloned.1.call-done = bf16[8192,128]{1,0:T(8,128)(2,1)} async-done(((bf16[2048,128]{1,0:T(8,128)(2,1)}), bf16[8192,128]{1,0:T(8,128)(2,1)}) %all-gather.11.cloned.1.call-update) | async-done | bytes 2097168 | tf_op jit(solution)/shard_map/all_gather | solution.py:36
  144.3 4.1 fusion.11
  148.4 0.0 copy-start.1
  148.4 32.8 %all-gather.5.cloned.1.call-done = bf16[128,8192]{1,0:T(8,128)(2,1)} async-done(((bf16[128,2048]{1,0:T(8,128)(2,1)}), bf16[128,8192]{1,0:T(8,128)(2,1)}) %all-gather.5.cloned.1.call-update) | async-done | bytes 2097168 | tf_op jit(solution)/shard_map/all_gather | solution.py:9
  181.2 4.1 multiply_convert_fusion.1
  185.3 2.8 fusion.12
  188.2 0.0 copy-done.1
  188.2 4.5 %convolution_add_fusion = f32[256,8192]{1,0:T(8,128)} fusion(f32[256,8192]{1,0:T(8,128)S(1)} %fusion.12, bf16[256,128]{1,0:T(8,128)(2,1)S(1)} %get-tuple-element.11, bf16[8192,128]{1,0:T(8,128)(2,1)S(1)} %copy-done.1), kind=kOutput, calls=%fused_computation.1 | convolution fusion | flops 538968064 | bytes 18939904 | tf_op jit(solution)/shard_map/dot_general | solution.py:57
  192.7 0.0 reduce-scatter.3.cloned.1.call-update
  192.7 0.0 reduce-scatter.5.cloned.1.call-start
  192.8 3.2 convolution_multiply_fusion
  196.0 0.3 copy-done
  196.2 0.8 fusion
  197.0 0.8 fusion.1
  197.8 5.0 %pad_maximum_fusion = f32[8192,384]{0,1:T(8,128)} fusion(f32[8192,128]{0,1:T(8,128)S(1)} %convolution_multiply_fusion, f32[8192,128]{0,1:T(8,128)S(1)} %fusion, f32[8192,128]{0,1:T(8,128)S(1)} %fusion.1), kind=kLoop, calls=%fused_computation | loop fusion | flops 6291456 | bytes 25165824 | tf_op jit(solution)/shard_map/concatenate | solution.py:64
  202.8 0.0 reduce-scatter.5.cloned.1.call-update
  202.8 79.6 %reduce-scatter.3.cloned.1.call-done = f32[256,1024]{1,0:T(8,128)} async-done(((f32[256,8192]{1,0:T(8,128)}), f32[256,1024]{1,0:T(8,128)}) %reduce-scatter.3.cloned.1.call-update) | async-done | bytes 1048592 | tf_op jit(solution)/shard_map/reduce_scatter | solution.py:58
  282.4 2.1 convert_element_type.14
  284.5 120.0 %reduce-scatter.5.cloned.1.call-done = f32[2048,384]{0,1:T(8,128)} async-done(((f32[8192,384]{0,1:T(8,128)}), f32[2048,384]{0,1:T(8,128)}) %reduce-scatter.5.cloned.1.call-update) | async-done | bytes 3145744 | tf_op jit(solution)/shard_map/reduce_scatter | solution.py:15
  404.5 3.1 slice_bitcast_fusion
  407.5 1.3 copy.10
  408.8 1.3 copy.9
  (3 shorter events, 0.0 us)
Async XLA Ops:
  7.2 107.5 %copy-start.2 = (bf16[256,1024]{1,0:T(8,128)(2,1)S(1)}, bf16[256,1024]{1,0:T(8,128)(2,1)}, u32[]{:S(2)}) copy-start(bf16[256,1024]{1,0:T(8,128)(2,1)} %param.6) | copy-start | bytes 1572868
  7.2 117.3 %all-gather.9.cloned.1.call-start = ((), (), s32[]{:S(2)}) async-start(), calls=%async_computation.4 | async-start | bytes 2621440 | tf_op jit(solution)/shard_map/all_gather | solution.py:37
  7.9 116.6 %all-gather.7.cloned.1.call-start = ((), (), s32[]{:S(2)}) async-start(), calls=%async_computation.3 | async-start | bytes 4718592 | tf_op jit(solution)/shard_map/all_gather | solution.py:28
  8.7 135.6 %all-gather.11.cloned.1.call-start = ((), (), s32[]{:S(2)}) async-start(), calls=%async_computation.5 | async-start | bytes 2621440 | tf_op jit(solution)/shard_map/all_gather | solution.py:36
  8.7 11.6 %collective-permute-start = (bf16[256,1024]{1,0:T(8,128)(2,1)}, bf16[256,1024]{1,0:T(8,128)(2,1)S(1)}, u32[]{:S(2)}, u32[]{:S(2)}) collective-permute-start(bf16[256,1024]{1,0:T(8,128)(2,1)} %param.6), channel_id=1, source_target_pairs={{0,1},{1,2},{2,3},{3,4},{4,5},{5,6},{6,7},{7,0},{8,9},{9,10},{10,1... | collective-permute-start | bytes 1572872 | tf_op jit(solution)/shard_map/ppermute | solution.py:31
  9.4 171.8 %all-gather.5.cloned.1.call-start = ((), (), s32[]{:S(2)}) async-start(), calls=%async_computation.2 | async-start | bytes 2621440 | tf_op jit(solution)/shard_map/all_gather | solution.py:9
  20.4 10.4 %collective-permute-start.1 = (bf16[256,1024]{1,0:T(8,128)(2,1)S(1)}, bf16[256,1024]{1,0:T(8,128)(2,1)S(1)}, u32[]{:S(2)}, u32[]{:S(2)}) collective-permute-start(bf16[256,1024]{1,0:T(8,128)(2,1)S(1)} %collective-permute-done), channel_id=1, source_target_pairs={{0,1},{1,2},{2,3},{3,4},{4,5},{5,6},{6,7},{7,0},{8,9},{9,10},{10,1... | collective-permute-start | bytes 1572872 | tf_op jit(solution)/shard_map/ppermute | solution.py:31
  30.8 10.4 %collective-permute-start.2 = (bf16[256,1024]{1,0:T(8,128)(2,1)S(1)}, bf16[256,1024]{1,0:T(8,128)(2,1)S(1)}, u32[]{:S(2)}, u32[]{:S(2)}) collective-permute-start(bf16[256,1024]{1,0:T(8,128)(2,1)S(1)} %collective-permute-done.1), channel_id=1, source_target_pairs={{0,1},{1,2},{2,3},{3,4},{4,5},{5,6},{6,7},{7,0},{8,9},{9,10},{10,1... | collective-permute-start | bytes 1572872 | tf_op jit(solution)/shard_map/ppermute | solution.py:31
  41.2 10.4 %collective-permute-start.3 = (bf16[256,1024]{1,0:T(8,128)(2,1)S(1)}, bf16[256,1024]{1,0:T(8,128)(2,1)S(1)}, u32[]{:S(2)}, u32[]{:S(2)}) collective-permute-start(bf16[256,1024]{1,0:T(8,128)(2,1)S(1)} %collective-permute-done.2), channel_id=1, source_target_pairs={{0,1},{1,2},{2,3},{3,4},{4,5},{5,6},{6,7},{7,0},{8,9},{9,10},{10,1... | collective-permute-start | bytes 1572872 | tf_op jit(solution)/shard_map/ppermute | solution.py:31
  51.6 11.1 %collective-permute-start.4 = (bf16[256,1024]{1,0:T(8,128)(2,1)S(1)}, bf16[256,1024]{1,0:T(8,128)(2,1)S(1)}, u32[]{:S(2)}, u32[]{:S(2)}) collective-permute-start(bf16[256,1024]{1,0:T(8,128)(2,1)S(1)} %collective-permute-done.3), channel_id=1, source_target_pairs={{0,1},{1,2},{2,3},{3,4},{4,5},{5,6},{6,7},{7,0},{8,9},{9,10},{10,1... | collective-permute-start | bytes 1572872 | tf_op jit(solution)/shard_map/ppermute | solution.py:31
  62.7 21.9 %collective-permute-start.5 = (bf16[256,1024]{1,0:T(8,128)(2,1)S(1)}, bf16[256,1024]{1,0:T(8,128)(2,1)}, u32[]{:S(2)}, u32[]{:S(2)}) collective-permute-start(bf16[256,1024]{1,0:T(8,128)(2,1)S(1)} %collective-permute-done.4), channel_id=1, source_target_pairs={{0,1},{1,2},{2,3},{3,4},{4,5},{5,6},{6,7},{7,0},{8,9},{9,10},{10,1... | collective-permute-start | bytes 1572872 | tf_op jit(solution)/shard_map/ppermute | solution.py:31
  84.5 22.1 %collective-permute-start.6 = (bf16[256,1024]{1,0:T(8,128)(2,1)}, bf16[256,1024]{1,0:T(8,128)(2,1)}, u32[]{:S(2)}, u32[]{:S(2)}) collective-permute-start(bf16[256,1024]{1,0:T(8,128)(2,1)} %collective-permute-done.5), channel_id=1, source_target_pairs={{0,1},{1,2},{2,3},{3,4},{4,5},{5,6},{6,7},{7,0},{8,9},{9,10},{10,1... | collective-permute-start | bytes 1572872 | tf_op jit(solution)/shard_map/ppermute | solution.py:31
  84.6 197.8 %reduce-scatter.3.cloned.1.call-start = ((), (), s32[]{:S(2)}) async-start(), calls=%async_computation.6 | async-start | bytes 9437184 | tf_op jit(solution)/shard_map/reduce_scatter | solution.py:58
  148.4 39.8 %copy-start.1 = (bf16[8192,128]{1,0:T(8,128)(2,1)S(1)}, bf16[8192,128]{1,0:T(8,128)(2,1)}, u32[]{:S(2)}) copy-start(bf16[8192,128]{1,0:T(8,128)(2,1)} %all-gather.9.cloned.1.call-done) | copy-start | bytes 6291460
  192.7 211.8 %reduce-scatter.5.cloned.1.call-start = ((), (), s32[]{:S(2)}) async-start(), calls=%async_computation.7 | async-start | bytes 15728640 | tf_op jit(solution)/shard_map/reduce_scatter | solution.py:15
  192.8 3.5 copy-start
Sparse Core Ops, SparseCore 0:
  9.8 37.8 all-gather.8
  49.4 59.2 all-gather.6
  110.5 33.7 all-gather.10
  146.0 35.1 all-gather.4
  192.8 89.5 reduce-scatter.2
  285.3 119.0 reduce-scatter.4
